TPU v7x, 128 devices: a whole 4x4x4 slice. The times are simulated.
128 devices in a mesh: dp: 16 (over y, x_lo, core), shard: 8 (over z, x_hi).
Axes of the slice: x: 4 (x_hi: 2, x_lo: 2; x = x_hi * 2 + x_lo), y: 4, z: 4, core: 2. Of those that a mesh axis runs over, the one named last changes fastest.
Arguments:
- gradients: bfloat16 [16, 88, 512, 512], P('dp', 'shard'), may hold values from -60 to 60
- owners: int32 [8, 11], P('shard'), may hold values from 0 to 15, as said below
- block_param: int32 [88], replicated, may hold values from 0 to 6, never falling along the last dimension, each value on 1 to 25 neighbouring positions
- left_stat: float32 [32, 8, 512, 512], P('dp', 'shard'), may hold values from -4 to 8, as said below
- right_stat: float32 [32, 8, 512, 512], P('dp', 'shard'), may hold values from -4 to 8, as said below
- moment: float32 [32, 8, 512, 512], P('dp', 'shard'), may hold values from 0.5 to 50
- left_root: bfloat16 [32, 8, 512, 512], P('dp', 'shard'), may hold values from -1 to 3.5, as said below
- right_root: bfloat16 [32, 8, 512, 512], P('dp', 'shard'), may hold values from -1 to 3.5, as said below
Outputs:
- new_left: float32 [32, 8, 512, 512], P('dp', 'shard')
- new_right: float32 [32, 8, 512, 512], P('dp', 'shard')
- new_moment: float32 [32, 8, 512, 512], P('dp', 'shard')
- update: bfloat16 [88, 512, 512], P('shard')
Inputs may be any that keep to these rules, and one draw needn't show every extreme that they name: `owners`: in each row, no value occurs more than 2 times, and some value occurs exactly 2 times. `left_stat`: each slot's matrix is symmetric. `right_stat`: each slot's matrix is symmetric. `left_root`: each slot's matrix is symmetric. `right_root`: each slot's matrix is symmetric.
All inputs are finite; a program needn't handle non-finite values.
Results may differ from a plain program's by a relative error of at most 0.0058.
Values may be sent and summed in bfloat16 or wider, within the bound.
A program may use at most 192 MiB of HBM per device.

v0:
```python
import jax
import jax.numpy as jnp
from jax import lax
from jax.sharding import Mesh
from jax.sharding import PartitionSpec as P

NPARAM = 7
DP = ("dp_0", "dp_1", "dp_2")
SHARD = ("shard_0", "shard_1")
DP_SHARD = ("dp_0", "dp_1", "dp_2", "shard_0", "shard_1")
decay_rate = 0.95
tiny_value = 1e-06


def by_axis(x, axes):
    for axis in axes:
        x = lax.psum(x, axis)
    return x


def on_device(gradients, owners, block_param, left_stat, right_stat, moment, left_root, right_root):
    replicas = lax.axis_size(DP)
    capacity = left_stat.shape[0]
    blocks = gradients.shape[1]
    block_width = gradients.shape[3]
    device = lax.axis_index(DP)
    column = lax.axis_index(SHARD)
    owner_row = owners[0]
    counter = jnp.arange(blocks, dtype=jnp.int32)
    same_owner = owner_row[:, None] == owner_row[None, :]
    earlier = counter[None, :] < counter[:, None]
    places = owner_row * capacity + jnp.sum(jnp.where(same_owner & earlier, 1, 0), axis=1).astype(
        jnp.int32
    )
    slot_ids = jnp.arange(replicas * capacity, dtype=jnp.int32)
    matches = places[None, :] == slot_ids[:, None]
    source = jnp.min(jnp.where(matches, counter[None, :], blocks), axis=1)
    partials = gradients[0].astype(jnp.float32)
    row_share = lax.psum_scatter(partials, DP, scatter_dimension=1, tiled=True)
    share_padded = jnp.concatenate(
        [row_share, jnp.zeros((1,) + row_share.shape[1:], jnp.float32)], axis=0
    )
    outgoing = jnp.take(share_padded, source, axis=0).reshape(
        replicas, capacity, block_width // replicas, block_width
    )
    arrived = lax.all_to_all(outgoing, DP, split_axis=0, concat_axis=2, tiled=True)
    summed = arrived[0]
    left_gram = jnp.einsum("cij,ckj->cik", summed, summed, precision=lax.Precision.HIGHEST)
    right_gram = jnp.einsum("cji,cjk->cik", summed, summed, precision=lax.Precision.HIGHEST)
    new_left = decay_rate * left_stat + (1.0 - decay_rate) * left_gram[:, None]
    new_right = decay_rate * right_stat + (1.0 - decay_rate) * right_gram[:, None]
    new_moment = decay_rate * moment + (1.0 - decay_rate) * (summed * summed)[:, None]
    adam_step = summed / (jnp.sqrt(new_moment[:, 0]) + tiny_value)
    left_half = jnp.einsum(
        "cij,cjk->cik",
        left_root[:, 0],
        summed.astype(jnp.bfloat16),
        preferred_element_type=jnp.float32,
    ).astype(jnp.bfloat16)
    direction = jnp.einsum(
        "cij,cjk->cik", left_half, right_root[:, 0], preferred_element_type=jnp.float32
    )
    my_slots = lax.dynamic_slice_in_dim(matches, device * capacity, capacity, 0)
    local_params = lax.dynamic_slice_in_dim(block_param, column * blocks, blocks, 0)
    slot_param = jnp.sum(jnp.where(my_slots, local_params[None, :], 0), axis=1)
    is_live = jnp.any(my_slots, axis=1)
    param_ids = jnp.arange(NPARAM, dtype=jnp.int32)
    member = (slot_param[:, None] == param_ids[None, :]) & is_live[:, None]
    adam_squares = jnp.sum(adam_step * adam_step, axis=(1, 2))
    direction_squares = jnp.sum(direction * direction, axis=(1, 2))
    adam_local = jnp.sum(jnp.where(member, adam_squares[:, None], 0.0), axis=0)
    direction_local = jnp.sum(jnp.where(member, direction_squares[:, None], 0.0), axis=0)
    adam_norm, direction_norm = (by_axis(adam_local, DP_SHARD), by_axis(direction_local, DP_SHARD))
    graft_ratio = jnp.sqrt((adam_norm + tiny_value) / (direction_norm + tiny_value))
    slot_ratio = jnp.sum(jnp.where(member, graft_ratio[None, :], 0.0), axis=1)
    slot_update = (slot_ratio[:, None, None] * direction).astype(jnp.bfloat16)
    returned = lax.all_to_all(slot_update, DP, split_axis=1, concat_axis=0, tiled=True)
    pieces = jnp.take(returned, places, axis=0)
    update = lax.all_gather(pieces, DP, axis=1, tiled=True)
    return (new_left, new_right, new_moment, update)


def solution(mesh):
    finer = Mesh(
        mesh.devices.reshape(4, 2, 2, 4, 2), ("dp_0", "dp_1", "dp_2", "shard_0", "shard_1")
    )
    placed = (
        P(DP, SHARD, None, None),
        P(SHARD, None),
        P(),
        P(DP, SHARD, None, None),
        P(DP, SHARD, None, None),
        P(DP, SHARD, None, None),
        P(DP, SHARD, None, None),
        P(DP, SHARD, None, None),
    )
    return jax.shard_map(
        on_device,
        mesh=finer,
        in_specs=placed,
        out_specs=(
            P(DP, SHARD, None, None),
            P(DP, SHARD, None, None),
            P(DP, SHARD, None, None),
            P(SHARD, None, None),
        ),
        check_vma=False,
    )
```

profile of v0, /device:TPU:1, one launch (start us, length us, event | category | flops | bytes accessed | tf_op | source)
XLA Modules:
  0.0 309.6 jit_solution(17516869295652060086)
XLA Ops:
  7.2 0.0 copy-start
  7.2 0.0 reduce-scatter.2.cloned.1.call-start
  7.2 8.7 %bitcast_convert_fusion = f32[11,512,512]{2,1,0:T(8,128)} fusion(bf16[1,11,512,512]{3,2,1,0:T(8,128)(2,1)} %param.8), kind=kLoop, calls=%fused_computation.2 | loop fusion | flops 2883584 | bytes 17301504 | tf_op jit(solution)/shard_map/convert_element_type | solution.py:38
  15.9 0.0 copy-start.6
  15.9 0.0 reduce-scatter.2.cloned.1.call-update
  15.9 0.6 copy-done.6
  16.6 0.2 select_reduce_fusion.1
  16.7 0.1 select_reduce_fusion
  16.9 0.1 reduce_min.14
  17.0 130.2 %reduce-scatter.2.cloned.1.call-done = f32[11,32,512]{2,1,0:T(8,128)} async-done(((f32[11,512,512]{2,1,0:T(8,128)}), f32[11,32,512]{2,1,0:T(8,128)}) %reduce-scatter.2.cloned.1.call-update) | async-done | bytes 720912 | tf_op jit(solution)/shard_map/reduce_scatter | solution.py:39
  147.2 1.2 concatenate.3
  148.4 2.0 gather_fusion
  150.4 3.1 %broadcast_select_fusion = f32[16,2,32,512]{3,2,1,0:T(8,128)} fusion(f32[16,2,32,512]{3,2,1,0:T(8,128)} %bitcast.83, pred[16,2]{1,0:T(8,128)(4,1)S(1)} %compare_and_fusion), kind=kLoop, calls=%fused_computation.23 | loop fusion | flops 524288 | bytes 4194336 | tf_op jit(solution)/shard_map/jit(_take)/select_n | solution.py:43
  153.5 0.0 copy-start.5
  153.5 5.9 %all-to-all-start = ((f32[16,2,32,512]{3,2,1,0:T(8,128)}), f32[16,2,32,512]{3,2,1,0:T(8,128)S(1)}, u32[]{:S(2)}, u32[]{:S(2)}) async-start(f32[16,2,32,512]{3,2,1,0:T(8,128)} %broadcast_select_fusion), calls=%async_computation.1 | async-start | bytes 4194304 | tf_op jit(solution)/shard_map/all_to_all | solution.py:46
  159.3 0.0 copy-done.5
  159.3 0.1 dynamic_slice.7
  159.4 0.1 fusion.15
  159.5 0.1 select_reduce_fusion.5
  159.7 26.7 %all-to-all-done = f32[16,2,32,512]{3,2,1,0:T(8,128)S(1)} async-done(((f32[16,2,32,512]{3,2,1,0:T(8,128)}), f32[16,2,32,512]{3,2,1,0:T(8,128)S(1)}, u32[]{:S(2)}, u32[]{:S(2)}) %all-to-all-start) | async-done | bytes 2097184 | tf_op jit(solution)/shard_map/all_to_all | solution.py:46
  186.4 0.0 copy-start.2
  186.4 0.3 multiply_multiply_fusion
  186.6 1.1 copy-done.2
  187.7 0.2 copy.65
  187.9 0.0 copy-start.3
  188.0 2.0 copy.61
  189.9 0.3 copy-done.3
  190.2 2.8 sqrt_add_fusion
  192.9 0.0 copy-done
  193.0 4.0 %multiply_reduce_fusion = (f32[2]{0:T(128)S(1)}, f32[2,512,512]{2,1,0:T(8,128)}) fusion(bf16[2,1,512,512]{3,2,1,0:T(8,128)(2,1)S(1)} %copy-done, bf16[2,1,512,512]{3,2,1,0:T(8,128)(2,1)} %param.14, f32[2,512,512]{2,1,0:T(8,128)S(1)} %bitcast.79), kind=kOutput, calls=%fused_computation.14 | convolution fusion | flops 1075838976 | bytes 6291464 | tf_op jit(solution)/shard_map/cij,cjk->cik/dot_general | solution.py:60
  197.0 2.7 fusion.3
  199.6 0.1 select_reduce_fusion.4
  199.7 7.2 %all-reduce.2 = (f32[7]{0:T(128)S(1)}, f32[7]{0:T(128)S(1)}) all-reduce(f32[7]{0:T(128)S(1)} %get-tuple-element.25, f32[7]{0:T(128)S(1)} %get-tuple-element.24), channel_id=1, replica_groups=mesh['dp_0'=4,'dp_1'=2,'dp_2'=2,'shard_0'=4,'shard_1'=2] {'dp_0'}, use_global_device_ids=true, to_apply=%region_14.15 | all-reduce | flops 14 | bytes 112 | tf_op jit(solution)/shard_map/psum | solution.py:17
  206.9 3.8 %all-reduce.5 = (f32[7]{0:T(128)S(1)}, f32[7]{0:T(128)S(1)}) all-reduce(f32[7]{0:T(128)S(1)} %get-tuple-element.28, f32[7]{0:T(128)S(1)} %get-tuple-element.29), channel_id=1, replica_groups=mesh['dp_0'=4,'dp_1'=2,'dp_2'=2,'shard_0'=4,'shard_1'=2] {'dp_1'}, use_global_device_ids=true, to_apply=%region_15.16 | all-reduce | flops 14 | bytes 112 | tf_op jit(solution)/shard_map/psum | solution.py:17
  210.7 6.2 %all-reduce.4 = (f32[7]{0:T(128)S(1)}, f32[7]{0:T(128)S(1)}) all-reduce(f32[7]{0:T(128)S(1)} %get-tuple-element.34, f32[7]{0:T(128)S(1)} %get-tuple-element.35), channel_id=1, replica_groups=mesh['dp_0'=4,'dp_1'=2,'dp_2'=2,'shard_0'=4,'shard_1'=2] {'dp_2'}, use_global_device_ids=true, to_apply=%region_16.17 | all-reduce | flops 14 | bytes 112 | tf_op jit(solution)/shard_map/psum | solution.py:17
  216.9 8.7 %all-reduce.1 = (f32[7]{0:T(128)S(1)}, f32[7]{0:T(128)S(1)}) all-reduce(f32[7]{0:T(128)S(1)} %get-tuple-element.32, f32[7]{0:T(128)S(1)} %get-tuple-element.33), channel_id=1, replica_groups=mesh['dp_0'=4,'dp_1'=2,'dp_2'=2,'shard_0'=4,'shard_1'=2] {'shard_0'}, use_global_device_ids=true, to_apply=%region_17.18 | all-reduce | flops 14 | bytes 112 | tf_op jit(solution)/shard_map/psum | solution.py:17
  225.6 5.3 %all-reduce.3 = (f32[7]{0:T(128)S(1)}, f32[7]{0:T(128)S(1)}) all-reduce(f32[7]{0:T(128)S(1)} %get-tuple-element.26, f32[7]{0:T(128)S(1)} %get-tuple-element.27), channel_id=1, replica_groups=mesh['dp_0'=4,'dp_1'=2,'dp_2'=2,'shard_0'=4,'shard_1'=2] {'shard_1'}, use_global_device_ids=true, to_apply=%region_18.19 | all-reduce | flops 14 | bytes 112 | tf_op jit(solution)/shard_map/psum | solution.py:17
  230.9 0.2 select_reduce_fusion.2
  231.1 1.9 multiply_convert_fusion
  233.0 2.0 copy.69
  235.0 7.0 %all-to-all-start.1 = ((bf16[2,512,512]{2,0,1:T(2,128)(2,1)}), bf16[2,512,512]{2,0,1:T(2,128)(2,1)S(1)}, u32[]{:S(2)}, u32[]{:S(2)}) async-start(bf16[2,512,512]{2,0,1:T(2,128)(2,1)} %copy.69), calls=%async_computation.2 | async-start | bytes 2097152 | tf_op jit(solution)/shard_map/all_to_all | solution.py:77
  242.0 0.2 all-gather.2.cloned.1.call-start
  242.2 15.5 %all-to-all-done.1 = bf16[2,512,512]{2,0,1:T(2,128)(2,1)S(1)} async-done(((bf16[2,512,512]{2,0,1:T(2,128)(2,1)}), bf16[2,512,512]{2,0,1:T(2,128)(2,1)S(1)}, u32[]{:S(2)}, u32[]{:S(2)}) %all-to-all-start.1) | async-done | bytes 1048608 | tf_op jit(solution)/shard_map/all_to_all | solution.py:77
  257.7 0.2 copy.70
  257.9 0.1 copy.71
  258.0 0.6 gather_fusion.1
  258.6 0.8 broadcast_select_fusion.1
  259.4 0.0 all-gather.2.cloned.1.call-update
  259.4 0.0 copy-start.4
  259.4 6.1 %fusion = f32[2,1,512,512]{3,2,1,0:T(8,128)} fusion(f32[2,1,512,512]{3,2,1,0:T(8,128)} %param.12, f32[2,512,512]{2,1,0:T(8,128)S(1)} %bitcast.80), kind=kOutput, calls=%fused_computation.6 | convolution fusion | flops 3222798336 | bytes 6291456 | tf_op jit(solution)/shard_map/cji,cjk->cik/dot_general | solution.py:49
  265.6 0.0 copy-done.4
  265.6 5.0 %fusion.1 = f32[2,1,512,512]{3,2,1,0:T(8,128)} fusion(f32[2,1,512,512]{3,2,1,0:T(8,128)S(1)} %copy-done.4, f32[2,512,512]{2,1,0:T(8,128)S(1)} %bitcast.81), kind=kOutput, calls=%fused_computation.9 | convolution fusion | flops 3222798336 | bytes 6291456 | tf_op jit(solution)/shard_map/cij,ckj->cik/dot_general | solution.py:48
  270.6 26.5 %all-gather.2.cloned.1.call-done = bf16[11,512,512]{2,1,0:T(8,128)(2,1)} async-done(((bf16[11,32,512]{2,1,0:T(8,128)(2,1)}), bf16[11,512,512]{2,1,0:T(8,128)(2,1)}) %all-gather.2.cloned.1.call-update) | async-done | bytes 5767184 | tf_op jit(solution)/shard_map/all_gather | solution.py:79
  297.1 0.0 copy-start.1
  297.1 5.6 %copy.85 = bf16[11,512,512]{2,1,0:T(8,128)(2,1)} copy(bf16[11,512,512]{2,1,0:T(8,128)(2,1)} %all-gather.2.cloned.1.call-done) | data formatting | bytes 11534336
  302.7 0.0 copy-done.1
  (9 shorter events, 0.1 us)
Async XLA Ops:
  7.2 185.8 %copy-start = (bf16[2,1,512,512]{3,2,1,0:T(8,128)(2,1)S(1)}, bf16[2,1,512,512]{3,2,1,0:T(8,128)(2,1)}, u32[]{:S(2)}) copy-start(bf16[2,1,512,512]{3,2,1,0:T(8,128)(2,1)} %param.15) | copy-start | bytes 3145732
  7.2 140.0 %reduce-scatter.2.cloned.1.call-start = ((), (), s32[]{:S(2)}) async-start(), calls=%async_computation.3 | async-start | bytes 12255232 | tf_op jit(solution)/shard_map/reduce_scatter | solution.py:39
  15.9 0.7 copy-start.6
  153.5 5.9 %copy-start.5 = (s32[88]{0:T(128)S(1)}, s32[88]{0:T(128)}, u32[]{:S(2)}) copy-start(s32[88]{0:T(128)} %param.10) | copy-start | bytes 1060
  153.5 32.9 %all-to-all-start = ((f32[16,2,32,512]{3,2,1,0:T(8,128)}), f32[16,2,32,512]{3,2,1,0:T(8,128)S(1)}, u32[]{:S(2)}, u32[]{:S(2)}) async-start(f32[16,2,32,512]{3,2,1,0:T(8,128)} %broadcast_select_fusion), calls=%async_computation.1 | async-start | bytes 4194304 | tf_op jit(solution)/shard_map/all_to_all | solution.py:46
  186.4 1.3 copy-start.2
  187.9 2.2 copy-start.3
  235.0 22.7 %all-to-all-start.1 = ((bf16[2,512,512]{2,0,1:T(2,128)(2,1)}), bf16[2,512,512]{2,0,1:T(2,128)(2,1)S(1)}, u32[]{:S(2)}, u32[]{:S(2)}) async-start(bf16[2,512,512]{2,0,1:T(2,128)(2,1)} %copy.69), calls=%async_computation.2 | async-start | bytes 2097152 | tf_op jit(solution)/shard_map/all_to_all | solution.py:77
  242.0 55.1 %all-gather.2.cloned.1.call-start = ((), (), s32[]{:S(2)}) async-start(), calls=%async_computation.4 | async-start | bytes 6127616 | tf_op jit(solution)/shard_map/all_gather | solution.py:79
  259.4 6.2 %copy-start.4 = (f32[2,1,512,512]{3,2,1,0:T(8,128)S(1)}, f32[2,1,512,512]{3,2,1,0:T(8,128)}, u32[]{:S(2)}) copy-start(f32[2,1,512,512]{3,2,1,0:T(8,128)} %param.11) | copy-start | bytes 6291460
  297.1 5.6 %copy-start.1 = (bf16[2,1,512,512]{3,2,1,0:T(8,128)(2,1)S(1)}, bf16[2,1,512,512]{3,2,1,0:T(8,128)(2,1)}, u32[]{:S(2)}) copy-start(bf16[2,1,512,512]{3,2,1,0:T(8,128)(2,1)} %param.15) | copy-start | bytes 3145732
Sparse Core Ops, SparseCore 0:
  16.0 131.0 reduce-scatter.1
  259.6 37.5 all-gather.1
where the time goes:
time: 310 us
  waiting for transfers between devices  199 us (64%)
  blocking collectives  31.1 us (10%)
  other arithmetic  21.1 us (7%)
  local copies, waits for them, and re-layouts  16 us (5%)
  matrix products  15.1 us (5%)
  between operations  14.2 us (5%)
  starting transfers between devices  13.1 us (4%)
    reduce_scatter x1, waiting for transfers between devices, on_device(): row_share = lax.psum_scatter(partials, DP, scatter_dimension=1, tiled=True)  130 us
    psum x5, blocking collectives, by_axis(): x = lax.psum(x, axis)  31.1 us
    all_to_all x1, waiting for transfers between devices, on_device(): lax.all_to_all(outgoing, DP, split_axis=0, concat_axis=2, tiled=True)  26.7 us
    all_gather x1, waiting for transfers between devices, on_device(): update = lax.all_gather(pieces, DP, axis=1, tiled=True)  26.5 us
    all_to_all x1, waiting for transfers between devices, on_device(): lax.all_to_all(slot_update, DP, split_axis=1, concat_axis=0, tiled=True)  15.5 us
    convert_element_type x1, other arithmetic, on_device(): partials = gradients[0].astype(jnp.float32)  8.67 us
    unnamed x15, local copies, waits for them, and re-layouts  7.59 us
    all_to_all x1, starting transfers between devices, on_device(): lax.all_to_all(slot_update, DP, split_axis=1, concat_axis=0, tiled=True)  6.96 us
  transfers between devices with their start and end apart: 4, of which 4 were waited for; matrix products, arithmetic and copies ran while one was open for 4% of the time, Pallas kernels for 0%

commit v1 on v0

--- a/solution.py
+++ b/solution.py
@@ -76,7 +76,8 @@
     slot_update = (slot_ratio[:, None, None] * direction).astype(jnp.bfloat16)
     returned = lax.all_to_all(slot_update, DP, split_axis=1, concat_axis=0, tiled=True)
     pieces = jnp.take(returned, places, axis=0)
-    update = lax.all_gather(pieces, DP, axis=1, tiled=True)
+    outgoing_2 = jnp.stack([pieces] * lax.axis_size(DP))
+    update = jnp.concatenate(lax.all_to_all(outgoing_2, DP, 0, 0), axis=1)
     return (new_left, new_right, new_moment, update)
 
 

time: 310 us -> 347 us (1.12)
  waiting for transfers between devices: 199 us -> 228 us
  starting transfers between devices: 13.1 us -> 18.2 us
  local copies, waits for them, and re-layouts: 16 us -> 19.9 us
    all_to_all x0 -> x1, waiting for transfers between devices: none -> 55.3 us  [on_device(): update = jnp.concatenate(lax.all_to_all(outgoing_2, DP, 0, 0), axis=1)]
    all_gather x1 -> x0, waiting for transfers between devices: 26.5 us -> none  [on_device(): update = lax.all_gather(pieces, DP, axis=1, tiled=True)]
    all_to_all x0 -> x1, local copies, waits for them, and re-layouts: none -> 6.25 us  [on_device(): update = jnp.concatenate(lax.all_to_all(outgoing_2, DP, 0, 0), axis=1)]
    unnamed x15 -> x14, local copies, waits for them, and re-layouts: 7.59 us -> 1.96 us
    all_to_all x0 -> x1, starting transfers between devices: none -> 5.3 us  [on_device(): update = jnp.concatenate(lax.all_to_all(outgoing_2, DP, 0, 0), axis=1)]
  transfers between devices with their start and end apart: 4 -> 4, of which waited for: 4 -> 4; matrix products, arithmetic and copies ran while one was open for 4% -> 3% of each run, Pallas kernels for 0% -> 0%
where the time goes in v1:
time: 347 us
  waiting for transfers between devices  228 us (66%)
  blocking collectives  31.1 us (9%)
  other arithmetic  20.4 us (6%)
  local copies, waits for them, and re-layouts  19.9 us (6%)
  starting transfers between devices  18.2 us (5%)
  matrix products  15.1 us (4%)
  between operations  14.2 us (4%)
    reduce_scatter x1, waiting for transfers between devices, on_device(): row_share = lax.psum_scatter(partials, DP, scatter_dimension=1, tiled=True)  130 us
    all_to_all x1, waiting for transfers between devices, on_device(): update = jnp.concatenate(lax.all_to_all(outgoing_2, DP, 0, 0), axis=1)  55.3 us
    psum x5, blocking collectives, by_axis(): x = lax.psum(x, axis)  31.1 us
    all_to_all x1, waiting for transfers between devices, on_device(): lax.all_to_all(outgoing, DP, split_axis=0, concat_axis=2, tiled=True)  26.7 us
    all_to_all x1, waiting for transfers between devices, on_device(): lax.all_to_all(slot_update, DP, split_axis=1, concat_axis=0, tiled=True)  15.7 us
    convert_element_type x1, other arithmetic, on_device(): partials = gradients[0].astype(jnp.float32)  8.67 us
    all_to_all x1, starting transfers between devices, on_device(): lax.all_to_all(slot_update, DP, split_axis=1, concat_axis=0, tiled=True)  6.96 us
  transfers between devices with their start and end apart: 4, of which 4 were waited for; matrix products, arithmetic and copies ran while one was open for 3% of the time, Pallas kernels for 0%

profile of v1, /device:TPU:1, one launch (start us, length us, event | category | flops | bytes accessed | tf_op | source)
XLA Modules:
  0.0 346.8 jit_solution(11973509764930689594)
XLA Ops:
  7.2 0.0 copy-start
  7.2 0.0 reduce-scatter.2.cloned.1.call-start
  7.2 8.7 %bitcast_convert_fusion = f32[11,512,512]{2,1,0:T(8,128)} fusion(bf16[1,11,512,512]{3,2,1,0:T(8,128)(2,1)} %param.8), kind=kLoop, calls=%fused_computation.2 | loop fusion | flops 2883584 | bytes 17301504 | tf_op jit(solution)/shard_map/convert_element_type | solution.py:38
  15.9 0.0 copy-start.6
  15.9 0.0 reduce-scatter.2.cloned.1.call-update
  15.9 0.6 copy-done.6
  16.6 0.2 select_reduce_fusion.1
  16.7 0.1 select_reduce_fusion
  16.9 0.1 reduce_min.14
  17.0 130.2 %reduce-scatter.2.cloned.1.call-done = f32[11,32,512]{2,1,0:T(8,128)} async-done(((f32[11,512,512]{2,1,0:T(8,128)}), f32[11,32,512]{2,1,0:T(8,128)}) %reduce-scatter.2.cloned.1.call-update) | async-done | bytes 720912 | tf_op jit(solution)/shard_map/reduce_scatter | solution.py:39
  147.2 1.2 concatenate.3
  148.4 2.0 gather_fusion
  150.4 3.1 broadcast_select_fusion
  153.5 0.0 copy-start.5
  153.5 5.9 %all-to-all-start = ((f32[16,2,32,512]{3,2,1,0:T(8,128)}), f32[16,2,32,512]{3,2,1,0:T(8,128)S(1)}, u32[]{:S(2)}, u32[]{:S(2)}) async-start(f32[16,2,32,512]{3,2,1,0:T(8,128)} %broadcast_select_fusion), calls=%async_computation.1 | async-start | bytes 4194304 | tf_op jit(solution)/shard_map/all_to_all | solution.py:46
  159.3 0.0 copy-done.5
  159.3 0.1 dynamic_slice.7
  159.4 0.1 fusion.15
  159.5 0.1 select_reduce_fusion.5
  159.7 26.7 %all-to-all-done = f32[16,2,32,512]{3,2,1,0:T(8,128)S(1)} async-done(((f32[16,2,32,512]{3,2,1,0:T(8,128)}), f32[16,2,32,512]{3,2,1,0:T(8,128)S(1)}, u32[]{:S(2)}, u32[]{:S(2)}) %all-to-all-start) | async-done | bytes 2097184 | tf_op jit(solution)/shard_map/all_to_all | solution.py:46
  186.4 0.0 copy-start.2
  186.4 0.3 multiply_multiply_fusion
  186.6 1.1 copy-done.2
  187.7 0.2 copy.66
  187.9 0.0 copy-start.3
  188.0 2.0 copy.62
  189.9 0.3 copy-done.3
  190.2 2.8 sqrt_add_fusion
  192.9 0.0 copy-done
  193.0 4.0 %multiply_reduce_fusion = (f32[2]{0:T(128)S(1)}, f32[2,512,512]{2,1,0:T(8,128)}) fusion(bf16[2,1,512,512]{3,2,1,0:T(8,128)(2,1)S(1)} %copy-done, bf16[2,1,512,512]{3,2,1,0:T(8,128)(2,1)} %param.14, f32[2,512,512]{2,1,0:T(8,128)S(1)} %bitcast.82), kind=kOutput, calls=%fused_computation.14 | convolution fusion | flops 1075838976 | bytes 6291464 | tf_op jit(solution)/shard_map/cij,cjk->cik/dot_general | solution.py:60
  197.0 2.7 fusion.3
  199.6 0.1 select_reduce_fusion.4
  199.7 7.2 %all-reduce.2 = (f32[7]{0:T(128)S(1)}, f32[7]{0:T(128)S(1)}) all-reduce(f32[7]{0:T(128)S(1)} %get-tuple-element.25, f32[7]{0:T(128)S(1)} %get-tuple-element.24), channel_id=1, replica_groups=mesh['dp_0'=4,'dp_1'=2,'dp_2'=2,'shard_0'=4,'shard_1'=2] {'dp_0'}, use_global_device_ids=true, to_apply=%region_14.15 | all-reduce | flops 14 | bytes 112 | tf_op jit(solution)/shard_map/psum | solution.py:17
  206.9 3.8 %all-reduce.5 = (f32[7]{0:T(128)S(1)}, f32[7]{0:T(128)S(1)}) all-reduce(f32[7]{0:T(128)S(1)} %get-tuple-element.28, f32[7]{0:T(128)S(1)} %get-tuple-element.29), channel_id=1, replica_groups=mesh['dp_0'=4,'dp_1'=2,'dp_2'=2,'shard_0'=4,'shard_1'=2] {'dp_1'}, use_global_device_ids=true, to_apply=%region_15.16 | all-reduce | flops 14 | bytes 112 | tf_op jit(solution)/shard_map/psum | solution.py:17
  210.7 6.2 %all-reduce.4 = (f32[7]{0:T(128)S(1)}, f32[7]{0:T(128)S(1)}) all-reduce(f32[7]{0:T(128)S(1)} %get-tuple-element.34, f32[7]{0:T(128)S(1)} %get-tuple-element.35), channel_id=1, replica_groups=mesh['dp_0'=4,'dp_1'=2,'dp_2'=2,'shard_0'=4,'shard_1'=2] {'dp_2'}, use_global_device_ids=true, to_apply=%region_16.17 | all-reduce | flops 14 | bytes 112 | tf_op jit(solution)/shard_map/psum | solution.py:17
  216.9 8.7 %all-reduce.1 = (f32[7]{0:T(128)S(1)}, f32[7]{0:T(128)S(1)}) all-reduce(f32[7]{0:T(128)S(1)} %get-tuple-element.32, f32[7]{0:T(128)S(1)} %get-tuple-element.33), channel_id=1, replica_groups=mesh['dp_0'=4,'dp_1'=2,'dp_2'=2,'shard_0'=4,'shard_1'=2] {'shard_0'}, use_global_device_ids=true, to_apply=%region_17.18 | all-reduce | flops 14 | bytes 112 | tf_op jit(solution)/shard_map/psum | solution.py:17
  225.6 5.3 %all-reduce.3 = (f32[7]{0:T(128)S(1)}, f32[7]{0:T(128)S(1)}) all-reduce(f32[7]{0:T(128)S(1)} %get-tuple-element.26, f32[7]{0:T(128)S(1)} %get-tuple-element.27), channel_id=1, replica_groups=mesh['dp_0'=4,'dp_1'=2,'dp_2'=2,'shard_0'=4,'shard_1'=2] {'shard_1'}, use_global_device_ids=true, to_apply=%region_18.19 | all-reduce | flops 14 | bytes 112 | tf_op jit(solution)/shard_map/psum | solution.py:17
  230.9 0.2 select_reduce_fusion.2
  231.1 1.9 multiply_convert_fusion
  233.0 2.0 copy.70
  235.0 7.0 %all-to-all-start.1 = ((bf16[2,512,512]{2,0,1:T(2,128)(2,1)}), bf16[2,512,512]{2,0,1:T(2,128)(2,1)S(1)}, u32[]{:S(2)}, u32[]{:S(2)}) async-start(bf16[2,512,512]{2,0,1:T(2,128)(2,1)} %copy.70), calls=%async_computation.2 | async-start | bytes 2097152 | tf_op jit(solution)/shard_map/all_to_all | solution.py:77
  242.0 15.7 %all-to-all-done.1 = bf16[2,512,512]{2,0,1:T(2,128)(2,1)S(1)} async-done(((bf16[2,512,512]{2,0,1:T(2,128)(2,1)}), bf16[2,512,512]{2,0,1:T(2,128)(2,1)S(1)}, u32[]{:S(2)}, u32[]{:S(2)}) %all-to-all-start.1) | async-done | bytes 1048608 | tf_op jit(solution)/shard_map/all_to_all | solution.py:77
  257.7 0.2 copy.71
  257.9 0.1 copy.72
  258.0 0.6 gather_fusion.1
  258.6 0.1 broadcast_select_fusion.1
  258.7 3.3 stack.2
  261.9 5.3 %all-to-all-start.2 = ((bf16[16,11,32,512]{3,2,1,0:T(8,128)(2,1)}), bf16[16,11,32,512]{3,2,1,0:T(8,128)(2,1)}, u32[]{:S(2)}, u32[]{:S(2)}) async-start(bf16[16,11,32,512]{3,2,1,0:T(8,128)(2,1)} %stack.2), calls=%async_computation.3 | async-start | bytes 11534336 | tf_op jit(solution)/shard_map/all_to_all | solution.py:80
  267.2 0.0 copy-start.4
  267.2 6.1 %fusion = f32[2,1,512,512]{3,2,1,0:T(8,128)} fusion(f32[2,1,512,512]{3,2,1,0:T(8,128)} %param.12, f32[2,512,512]{2,1,0:T(8,128)S(1)} %bitcast.83), kind=kOutput, calls=%fused_computation.6 | convolution fusion | flops 3222798336 | bytes 6291456 | tf_op jit(solution)/shard_map/cji,cjk->cik/dot_general | solution.py:49
  273.4 0.0 copy-done.4
  273.4 5.0 %fusion.1 = f32[2,1,512,512]{3,2,1,0:T(8,128)} fusion(f32[2,1,512,512]{3,2,1,0:T(8,128)S(1)} %copy-done.4, f32[2,512,512]{2,1,0:T(8,128)S(1)} %bitcast.84), kind=kOutput, calls=%fused_computation.9 | convolution fusion | flops 3222798336 | bytes 6291456 | tf_op jit(solution)/shard_map/cij,ckj->cik/dot_general | solution.py:48
  278.4 55.3 %all-to-all-done.2 = bf16[16,11,32,512]{3,2,1,0:T(8,128)(2,1)} async-done(((bf16[16,11,32,512]{3,2,1,0:T(8,128)(2,1)}), bf16[16,11,32,512]{3,2,1,0:T(8,128)(2,1)}, u32[]{:S(2)}, u32[]{:S(2)}) %all-to-all-start.2) | async-done | bytes 5767200 | tf_op jit(solution)/shard_map/all_to_all | solution.py:80
  333.7 0.0 copy-start.1
  333.7 6.2 %copy.73 = bf16[16,11,32,512]{3,2,0,1:T(8,128)(2,1)} copy(bf16[16,11,32,512]{3,2,1,0:T(8,128)(2,1)} %all-to-all-done.2) | data formatting | bytes 11534336 | tf_op jit(solution)/shard_map/all_to_all | solution.py:80
  340.0 0.0 copy-done.1
  (9 shorter events, 0.1 us)
Async XLA Ops:
  7.2 185.8 %copy-start = (bf16[2,1,512,512]{3,2,1,0:T(8,128)(2,1)S(1)}, bf16[2,1,512,512]{3,2,1,0:T(8,128)(2,1)}, u32[]{:S(2)}) copy-start(bf16[2,1,512,512]{3,2,1,0:T(8,128)(2,1)} %param.15) | copy-start | bytes 3145732
  7.2 140.0 %reduce-scatter.2.cloned.1.call-start = ((), (), s32[]{:S(2)}) async-start(), calls=%async_computation.4 | async-start | bytes 12255232 | tf_op jit(solution)/shard_map/reduce_scatter | solution.py:39
  15.9 0.7 copy-start.6
  153.5 5.9 %copy-start.5 = (s32[88]{0:T(128)S(1)}, s32[88]{0:T(128)}, u32[]{:S(2)}) copy-start(s32[88]{0:T(128)} %param.10) | copy-start | bytes 1060
  153.5 32.9 %all-to-all-start = ((f32[16,2,32,512]{3,2,1,0:T(8,128)}), f32[16,2,32,512]{3,2,1,0:T(8,128)S(1)}, u32[]{:S(2)}, u32[]{:S(2)}) async-start(f32[16,2,32,512]{3,2,1,0:T(8,128)} %broadcast_select_fusion), calls=%async_computation.1 | async-start | bytes 4194304 | tf_op jit(solution)/shard_map/all_to_all | solution.py:46
  186.4 1.3 copy-start.2
  187.9 2.2 copy-start.3
  235.0 22.7 %all-to-all-start.1 = ((bf16[2,512,512]{2,0,1:T(2,128)(2,1)}), bf16[2,512,512]{2,0,1:T(2,128)(2,1)S(1)}, u32[]{:S(2)}, u32[]{:S(2)}) async-start(bf16[2,512,512]{2,0,1:T(2,128)(2,1)} %copy.70), calls=%async_computation.2 | async-start | bytes 2097152 | tf_op jit(solution)/shard_map/all_to_all | solution.py:77
  261.9 71.8 %all-to-all-start.2 = ((bf16[16,11,32,512]{3,2,1,0:T(8,128)(2,1)}), bf16[16,11,32,512]{3,2,1,0:T(8,128)(2,1)}, u32[]{:S(2)}, u32[]{:S(2)}) async-start(bf16[16,11,32,512]{3,2,1,0:T(8,128)(2,1)} %stack.2), calls=%async_computation.3 | async-start | bytes 11534336 | tf_op jit(solution)/shard_map/all_to_all | solution.py:80
  267.2 6.1 %copy-start.4 = (f32[2,1,512,512]{3,2,1,0:T(8,128)S(1)}, f32[2,1,512,512]{3,2,1,0:T(8,128)}, u32[]{:S(2)}) copy-start(f32[2,1,512,512]{3,2,1,0:T(8,128)} %param.11) | copy-start | bytes 6291460
  333.7 6.2 %copy-start.1 = (bf16[2,1,512,512]{3,2,1,0:T(8,128)(2,1)S(1)}, bf16[2,1,512,512]{3,2,1,0:T(8,128)(2,1)}, u32[]{:S(2)}) copy-start(bf16[2,1,512,512]{3,2,1,0:T(8,128)(2,1)} %param.15) | copy-start | bytes 3145732
Sparse Core Ops, SparseCore 0:
  16.0 131.0 reduce-scatter.1
